TPU v7x, 32 devices: a whole 2x2x4 slice. The times are simulated.
32 devices in a mesh: dp: 8 (over z, y), mp: 4 (over x, core).
Axes of the slice: x: 2, y: 2, z: 4, core: 2. Of those that a mesh axis runs over, the one named last changes fastest.
Arguments:
- streams: bfloat16 [2048, 4, 8192], P('dp', None, 'mp'), may hold values from -200 to 200
- branch_out: bfloat16 [2048, 8192], P('dp', 'mp'), may hold values from -6 to 6
- merge_weight: float32 [20, 4, 8192], P(None, None, ('mp', 'dp')), may hold values from -0.03125 to 0.03125
- next_weight: float32 [24, 4, 8192], P(None, None, ('mp', 'dp')), may hold values from -0.03125 to 0.03125
- blend_bias: float32 [44], replicated, may hold values from -3 to 3
- blend_scale: float32 [5], replicated, may hold values from 0.5 to 3
- norm_gain: float32 [8192], P('mp'), may hold values from 0.5 to 1.5
Outputs:
- streams_out: bfloat16 [2048, 4, 8192], P('dp', None, 'mp')
- branch_in: bfloat16 [2048, 8192], P('dp', 'mp')
- next_mix: float32 [2048, 20], P('dp')
All inputs are finite; a program needn't handle non-finite values.
Results may differ from a plain program's by a relative error of at most 0.001.
Values sent between devices are 32-bit elements; how exact they have to be, the bound alone decides.
No kernel may reach another device: no remote copies, remote signals or barrier semaphores. Data moves between devices by JAX's collectives and lax.ppermute only.
A program may use at most 64 MiB of HBM per device.

v0:
```python
import jax
import jax.numpy as jnp
from jax import lax
from jax.sharding import PartitionSpec as P

D = 8192
STREAMS = 4
BALANCE_ROUNDS = 6
epsilon = 1e-06


def balance_normalize(balanced_matrix):
    for balance_round in range(BALANCE_ROUNDS):
        balanced_matrix = balanced_matrix / jnp.sum(balanced_matrix, axis=2, keepdims=True)
        balanced_matrix = balanced_matrix / jnp.sum(balanced_matrix, axis=1, keepdims=True)
    return balanced_matrix


def settle(columns, finish):
    summed = lax.psum(columns, "mp")
    result = finish(summed)
    return result


def first_coef(raw_sums, squares, blend_bias, blend_scale):
    rms_root = jnp.sqrt(squares / (STREAMS * D) + epsilon)
    score_logits = raw_sums / rms_root[:, None]
    post_mix = 2.0 * jax.nn.sigmoid(blend_scale[0] * score_logits[:, :4] + blend_bias[:4])
    residual_blend = balance_normalize(
        jnp.exp(
            blend_scale[1] * score_logits[:, 4:20].reshape(-1, 4, 4)
            + blend_bias[4:20].reshape(4, 4)
        )
    )
    return (post_mix, residual_blend)


def second_coef(raw_sums, squares, blend_bias, blend_scale):
    rms_root = jnp.sqrt(squares / (STREAMS * D) + epsilon)
    score_logits = raw_sums / rms_root[:, None]
    pre_next = jax.nn.sigmoid(blend_scale[2] * score_logits[:, :4] + blend_bias[20:24])
    post_next = 2.0 * jax.nn.sigmoid(blend_scale[3] * score_logits[:, 4:8] + blend_bias[24:28])
    residual_following = balance_normalize(
        jnp.exp(
            blend_scale[4] * score_logits[:, 8:24].reshape(-1, 4, 4)
            + blend_bias[28:44].reshape(4, 4)
        )
    )
    return (pre_next, post_next, residual_following)


def mix_streams(residual_blend, post_mix, streams, branch_out):
    branch_wide = branch_out.astype(jnp.float32)
    outputs = []
    for target in range(STREAMS):
        total = post_mix[:, target, None] * branch_wide
        for source in range(STREAMS):
            total = total + residual_blend[:, target, source, None] * streams[:, source, :].astype(
                jnp.float32
            )
        outputs.append(total)
    return jnp.stack(outputs, axis=1)


def unite(pre_next, mixed):
    total = pre_next[:, 0, None] * mixed[:, 0, :]
    for source in range(1, STREAMS):
        total = total + pre_next[:, source, None] * mixed[:, source, :]
    return total


def local(streams, branch_out, merge_weight, next_weight, blend_bias, blend_scale, norm_gain):
    merge_rows, next_rows = (
        lax.all_gather(merge_weight, "dp", axis=2, tiled=True),
        lax.all_gather(next_weight, "dp", axis=2, tiled=True),
    )
    highest = lax.Precision.HIGHEST
    raw_part = jnp.einsum(
        "tic,kic->tk", streams, merge_rows, precision=highest, preferred_element_type=jnp.float32
    )
    gram_part = jnp.einsum("tic,tjc->tij", streams, streams, preferred_element_type=jnp.float32)
    columns = jnp.concatenate([raw_part, jnp.trace(gram_part, axis1=1, axis2=2)[:, None]], axis=1)

    def finish_first(summed):
        post_mix, residual_blend = first_coef(
            summed[:, :20], summed[:, 20], blend_bias, blend_scale
        )
        return jnp.concatenate([post_mix, residual_blend.reshape(-1, 16)], axis=1)

    merge_coef = settle(columns, finish_first)
    post_mix = merge_coef[:, :4]
    residual_blend = merge_coef[:, 4:20].reshape(-1, 4, 4)
    mixed = mix_streams(residual_blend, post_mix, streams, branch_out)
    streams_out = mixed.astype(jnp.bfloat16)
    raw_next = jnp.einsum("tic,kic->tk", mixed, next_rows, precision=highest)
    extra_cols = jnp.sum(mixed * mixed, axis=(1, 2))[:, None]
    columns_next = jnp.concatenate([raw_next, extra_cols], axis=1)

    def finish_second(summed):
        squares = summed[:, 24]
        pre_next, post_next, residual_following = second_coef(
            summed[:, :24], squares, blend_bias, blend_scale
        )
        pieces = [pre_next, post_next, residual_following.reshape(-1, 16)]
        return jnp.concatenate(pieces, axis=1)

    next_coef = settle(columns_next, finish_second)
    pre_next = next_coef[:, :4]
    next_mix = next_coef[:, 4:24]
    united = unite(pre_next, mixed)
    united_sq = lax.psum(jnp.sum(united * united, axis=1), "mp")
    branch_in = (united / jnp.sqrt(united_sq / D + epsilon)[:, None] * norm_gain).astype(
        jnp.bfloat16
    )
    return (streams_out, branch_in, next_mix)


def solution(mesh):
    placed = (
        P("dp", None, "mp"),
        P("dp", "mp"),
        P(None, None, ("mp", "dp")),
        P(None, None, ("mp", "dp")),
        P(),
        P(),
        P("mp"),
    )
    return jax.shard_map(
        local,
        mesh=mesh,
        in_specs=placed,
        out_specs=(P("dp", None, "mp"), P("dp", "mp"), P("dp", None)),
        check_vma=False,
    )
```

profile of v0, /device:TPU:0, one launch (start us, length us, event | category | flops | bytes accessed | tf_op | source)
XLA Modules:
  0.0 152.0 jit_solution(15976659351027897930)
XLA Ops:
  0.6 0.0 copy-start.7
  0.7 0.0 copy-start.8
  0.7 0.0 copy-start.6
  0.7 0.0 copy-start.5
  0.7 9.4 %fusion.28 = f32[256]{0:T(256)S(1)} fusion(bf16[256,4,2048]{2,1,0:T(4,128)(2,1)} %param.7, pred[4,4]{1,0:T(4,128)(4,1)S(1)} %iota_compare_fusion), kind=kOutput, calls=%fused_computation.54 | convolution fusion | flops 16785152 | bytes 4195344 | tf_op jit(solution)/shard_map/tic,tjc->tij/dot_general | solution.py:81
  10.1 0.0 copy-done.7
  10.1 0.1 fusion.80
  10.2 0.1 add.136
  10.2 0.1 fusion.79
  10.3 0.1 add.168
  10.4 0.0 copy-done.8
  10.4 0.6 fusion.78
  11.0 0.0 copy-done.6
  11.0 0.0 copy-done.5
  11.1 33.9 %all_gather.7 = f32[24,4,2048]{2,0,1:T(8,128)S(1)} all-gather(f32[24,4,256]{2,0,1:T(8,128)S(1)} %copy.16), channel_id=1, replica_groups=mesh['dp'=8,'mp'=4] {'dp'}, dimensions={2}, use_global_device_ids=true | all-gather | bytes 884736 | tf_op jit(solution)/shard_map/all_gather | solution.py:75
  45.0 32.1 %all_gather.6 = f32[20,4,2048]{2,0,1:T(8,128)S(1)} all-gather(f32[20,4,256]{2,0,1:T(8,128)S(1)} %copy.10), channel_id=1, replica_groups=mesh['dp'=8,'mp'=4] {'dp'}, dimensions={2}, use_global_device_ids=true | all-gather | bytes 737280 | tf_op jit(solution)/shard_map/all_gather | solution.py:74
  77.1 9.2 %convolution_bitcast_fusion = f32[256,20]{0,1:T(8,128)S(1)} fusion(f32[20,4,2048]{2,0,1:T(8,128)S(1)} %all_gather.6, bf16[256,4,2048]{2,1,0:T(4,128)(2,1)} %param.7), kind=kOutput, calls=%fused_computation.56 | convolution fusion | flops 503316480 | bytes 4870144 | tf_op jit(solution)/shard_map/tic,kic->tk/dot_general | solution.py:78
  86.3 10.4 %psum.21 = f32[256,21]{0,1:T(8,128)S(1)} all-reduce(f32[256,21]{0,1:T(8,128)S(1)} %pad_maximum_fusion.5), channel_id=1, replica_groups=mesh['dp'=8,'mp'=4] {'mp'}, use_global_device_ids=true, to_apply=%region_1.2 | all-reduce | flops 5376 | bytes 43008 | tf_op jit(solution)/shard_map/psum | solution.py:20
  96.7 0.8 fusion.56
  97.5 0.7 slice_multiply_fusion.1
  98.2 0.1 fusion.74
  98.6 0.0 copy-start.4
  98.6 4.6 %copy.11 = bf16[256,4,2048]{2,0,1:T(8,128)(2,1)S(1)} copy(bf16[256,4,2048]{2,1,0:T(4,128)(2,1)} %param.7) | data formatting | bytes 8388608 | tf_op args[0]
  103.2 0.0 copy-done.4
  103.2 2.3 %fusion.13 = (f32[256,2048]{1,0:T(8,128)S(1)}, f32[256,2048]{1,0:T(8,128)S(1)}) fusion(bf16[256,2048]{1,0:T(8,128)(2,1)S(1)} %copy-done.4, f32[256]{0:T(256)S(1)} %bitcast.135, f32[256]{0:T(256)S(1)} %bitcast.136, f32[256]{0:T(256)S(1)} %bitcast.137, f32[256]{0:T(256)S(1)} %bitcast.130, f32[256]{0:T(256)S(1)} %bitcast.140, ...), kind=kLoop, calls=%fused_computation.35 | loop fusion | flops 12058624 | bytes 9447424 | tf_op jit(solution)/shard_map/add | solution.py:58
  105.5 0.0 copy-start
  105.5 2.3 %fusion.21 = (f32[256,2048]{1,0:T(8,128)S(1)}, f32[256,2048]{1,0:T(8,128)S(1)}) fusion(bf16[256,2048]{1,0:T(8,128)(2,1)S(1)} %copy-done.4, f32[256]{0:T(256)S(1)} %bitcast.126, f32[256]{0:T(256)S(1)} %bitcast.127, f32[256]{0:T(256)S(1)} %bitcast.128, f32[256]{0:T(256)S(1)} %bitcast.129, f32[256]{0:T(256)S(1)} %bitcast.139, ...), kind=kLoop, calls=%fused_computation.43 | loop fusion | flops 12058624 | bytes 9447424 | tf_op jit(solution)/shard_map/add | solution.py:58
  107.8 0.0 copy-start.2
  107.8 0.0 copy-start.3
  107.8 6.6 %fusion.29 = f32[256,24]{0,1:T(8,128)S(1)} fusion(f32[24,4,2048]{2,0,1:T(8,128)S(1)} %all_gather.7, f32[256,1,2048]{2,0,1:T(8,128)S(1)} %bitcast.111, f32[256,1,2048]{2,0,1:T(8,128)S(1)} %bitcast.108, f32[256,1,2048]{2,0,1:T(8,128)S(1)} %bitcast.105, f32[256,1,2048]{2,0,1:T(8,128)S(1)} %bitcast.102), kind=kOutput, calls=%fused_computation.55 | convolution fusion | flops 610271232 | bytes 9199616 | tf_op jit(solution)/shard_map/tic,kic->tk/dot_general | solution.py:95
  114.4 0.9 multiply_reduce_fusion
  115.3 10.8 %psum.22 = f32[256,25]{0,1:T(8,128)S(1)} all-reduce(f32[256,25]{0,1:T(8,128)S(1)} %pad_maximum_fusion.4), channel_id=1, replica_groups=mesh['dp'=8,'mp'=4] {'mp'}, use_global_device_ids=true, to_apply=%region_15.16 | all-reduce | flops 6400 | bytes 51200 | tf_op jit(solution)/shard_map/psum | solution.py:20
  126.1 1.4 fusion.45
  127.5 0.6 slice_multiply_fusion
  128.1 0.1 fusion.72
  128.2 0.1 divide_reduce_fusion
  128.3 0.1 divide_reduce_fusion.6
  128.4 0.1 divide_reduce_fusion.5
  128.5 0.1 divide_reduce_fusion.4
  128.7 0.1 divide_reduce_fusion.3
  128.8 0.1 divide_reduce_fusion.2
  128.9 0.7 exponential_divide_fusion
  129.6 0.6 pad_maximum_fusion.6
  130.2 4.9 %multiply_reduce_fusion.1 = (f32[256]{0:T(256)S(1)}, f32[256,2048]{1,0:T(8,128)}) fusion(f32[256,2048]{1,0:T(8,128)} %copy-done.3, f32[256]{0:T(256)S(1)} %bitcast.143, f32[256,2048]{1,0:T(8,128)} %copy-done.2, f32[256]{0:T(256)S(1)} %bitcast.144, f32[256,2048]{1,0:T(8,128)} %copy-done, f32[256]{0:T(256)S(1)} %bitcast.145, ...), kind=kLoop, calls=%fused_computation.49 | loop fusion | flops 4718336 | bytes 10490880 | tf_op jit(solution)/shard_map/reduce_sum | solution.py:111
  135.1 5.9 %psum.23 = f32[256]{0:T(256)S(1)} all-reduce(f32[256]{0:T(256)S(1)} %get-tuple-element.6), channel_id=1, replica_groups=mesh['dp'=8,'mp'=4] {'mp'}, use_global_device_ids=true, to_apply=%region_17.18 | all-reduce | flops 256 | bytes 2048 | tf_op jit(solution)/shard_map/psum | solution.py:111
  141.1 3.0 %multiply_convert_fusion = bf16[256,2048]{1,0:T(8,128)(2,1)} fusion(f32[256,2048]{1,0:T(8,128)} %get-tuple-element.7, f32[2048]{0:T(1024)S(1)} %copy-done.9, f32[256]{0:T(256)S(1)} %add_sqrt_fusion), kind=kLoop, calls=%fused_computation.48 | loop fusion | flops 1572864 | bytes 3154944 | tf_op jit(solution)/shard_map/convert_element_type | solution.py:112
  144.1 2.6 %fusion.27 = bf16[256,4,2048]{2,0,1:T(8,128)(2,1)S(1)} fusion(f32[256,1,2048]{2,0,1:T(8,128)} %bitcast.113, f32[256,1,2048]{2,0,1:T(8,128)} %bitcast.110, f32[256,1,2048]{2,0,1:T(8,128)S(1)} %bitcast.107, f32[256,1,2048]{2,0,1:T(8,128)S(1)} %bitcast.104), kind=kLoop, calls=%fused_computation.52 | loop fusion | flops 6291456 | bytes 12582912 | tf_op jit(solution)/shard_map/convert_element_type | solution.py:94
  146.7 5.3 %copy.17 = bf16[256,4,2048]{2,1,0:T(4,128)(2,1)} copy(bf16[256,4,2048]{2,0,1:T(8,128)(2,1)S(1)} %fusion.27) | data formatting | bytes 8388608
  (33 shorter events, 0.4 us)
Async XLA Ops:
  0.6 9.4 %copy-start.7 = (f32[44]{0:T(128)S(1)}, f32[44]{0:T(128)}, u32[]{:S(2)}) copy-start(f32[44]{0:T(128)} %param.11) | copy-start | bytes 532
  0.7 9.8 %copy-start.8 = (f32[5]{0:T(128)S(1)}, f32[5]{0:T(128)}, u32[]{:S(2)}) copy-start(f32[5]{0:T(128)} %param.12) | copy-start | bytes 64
  0.7 10.4 %copy-start.6 = (f32[20,4,256]{2,1,0:T(4,128)S(1)}, f32[20,4,256]{2,1,0:T(4,128)}, u32[]{:S(2)}) copy-start(f32[20,4,256]{2,1,0:T(4,128)} %param.9) | copy-start | bytes 245764
  0.7 10.4 %copy-start.5 = (f32[24,4,256]{2,1,0:T(4,128)S(1)}, f32[24,4,256]{2,1,0:T(4,128)}, u32[]{:S(2)}) copy-start(f32[24,4,256]{2,1,0:T(4,128)} %param.10) | copy-start | bytes 294916
  98.6 4.6 %copy-start.4 = (bf16[256,2048]{1,0:T(8,128)(2,1)S(1)}, bf16[256,2048]{1,0:T(8,128)(2,1)}, u32[]{:S(2)}) copy-start(bf16[256,2048]{1,0:T(8,128)(2,1)} %param.8) | copy-start | bytes 3145732
  105.5 8.9 %copy-start = (f32[256,2048]{1,0:T(8,128)}, f32[256,2048]{1,0:T(8,128)S(1)}, u32[]{:S(2)}) copy-start(f32[256,2048]{1,0:T(8,128)S(1)} %get-tuple-element.11) | copy-start | bytes 6291460
  107.8 6.6 %copy-start.2 = (f32[256,2048]{1,0:T(8,128)}, f32[256,2048]{1,0:T(8,128)S(1)}, u32[]{:S(2)}) copy-start(f32[256,2048]{1,0:T(8,128)S(1)} %get-tuple-element.12) | copy-start | bytes 6291460
  107.8 6.6 %copy-start.3 = (f32[256,2048]{1,0:T(8,128)}, f32[256,2048]{1,0:T(8,128)S(1)}, u32[]{:S(2)}) copy-start(f32[256,2048]{1,0:T(8,128)S(1)} %get-tuple-element.13) | copy-start | bytes 6291460
  130.2 10.8 %copy-start.9 = (f32[2048]{0:T(1024)S(1)}, f32[2048]{0:T(1024)}, u32[]{:S(2)}) copy-start(f32[2048]{0:T(1024)} %param.13) | copy-start | bytes 24580
  141.0 3.1 %copy-start.1 = (f32[256,2048]{1,0:T(8,128)S(1)}, f32[256,2048]{1,0:T(8,128)}, u32[]{:S(2)}) copy-start(f32[256,2048]{1,0:T(8,128)} %copy-done) | copy-start | bytes 6291460
where the time goes:
time: 152 us
  blocking collectives  93.1 us (61%)
  matrix products  25.2 us (17%)
  other arithmetic  21.8 us (14%)
  local copies, waits for them, and re-layouts  10.9 us (7%)
    all_gather x1, blocking collectives, local(): lax.all_gather(next_weight, 'dp', axis=2, tiled=True)  33.9 us
    all_gather x1, blocking collectives, local(): lax.all_gather(merge_weight, 'dp', axis=2, tiled=True)  32.1 us
    psum x2, blocking collectives, settle(): summed = lax.psum(columns, 'mp')  21.2 us
    unnamed x26, local copies, waits for them, and re-layouts  9.92 us
    dot_general x1, matrix products, local(): jnp.einsum('tic,tjc->tij', streams, streams, preferred_element_type=jnp.f...  9.4 us
    dot_general x1, matrix products, local(): jnp.einsum('tic,kic->tk', streams, merge_rows, precision=highest, preferr...  9.18 us
    dot_general x1, matrix products, local(): raw_next = jnp.einsum('tic,kic->tk', mixed, next_rows, precision=highest)  6.59 us
    psum x1, blocking collectives, local(): united_sq = lax.psum(jnp.sum(united * united, axis=1), 'mp')  5.92 us

commit v1 on v0

--- a/solution.py
+++ b/solution.py
@@ -17,7 +17,7 @@
 
 
 def settle(columns, finish):
-    summed = lax.psum(columns, "mp")
+    summed = jnp.sum(lax.all_gather(columns, "mp"), axis=0)
     result = finish(summed)
     return result
 

time: 152 us -> 144 us (0.947)
  blocking collectives: 93.1 us -> 84.2 us
    psum x2 -> x0, blocking collectives: 21.2 us -> none  [settle(): summed = lax.psum(columns, 'mp')]
    all_gather x0 -> x2, blocking collectives: none -> 11.1 us  [settle(): summed = jnp.sum(lax.all_gather(columns, 'mp'), axis=0)]
where the time goes in v1:
time: 144 us; the launch traced here: 143 us
  blocking collectives  84.2 us (58%)
  matrix products  25.2 us (18%)
  other arithmetic  21.9 us (15%)
  local copies, waits for them, and re-layouts  11 us (8%)
    all_gather x1, blocking collectives, local(): lax.all_gather(next_weight, 'dp', axis=2, tiled=True)  33.9 us
    all_gather x1, blocking collectives, local(): lax.all_gather(merge_weight, 'dp', axis=2, tiled=True)  32.1 us
    all_gather x2, blocking collectives, settle(): summed = jnp.sum(lax.all_gather(columns, 'mp'), axis=0)  11.1 us
    unnamed x26, local copies, waits for them, and re-layouts  9.92 us
    dot_general x1, matrix products, local(): jnp.einsum('tic,tjc->tij', streams, streams, preferred_element_type=jnp.f...  9.4 us
    dot_general x1, matrix products, local(): jnp.einsum('tic,kic->tk', streams, merge_rows, precision=highest, preferr...  9.18 us
    psum x1, blocking collectives, local(): united_sq = lax.psum(jnp.sum(united * united, axis=1), 'mp')  7.06 us
    dot_general x1, matrix products, local(): raw_next = jnp.einsum('tic,kic->tk', mixed, next_rows, precision=highest)  6.59 us

profile of v1, /device:TPU:0, one launch (start us, length us, event | category | flops | bytes accessed | tf_op | source)
XLA Modules:
  0.0 143.3 jit_solution(17689342849189123458)
XLA Ops:
  0.6 0.0 copy-start.7
  0.7 0.0 copy-start.8
  0.7 0.0 copy-start.6
  0.7 0.0 copy-start.5
  0.7 9.4 %fusion.28 = f32[256]{0:T(256)S(1)} fusion(bf16[256,4,2048]{2,1,0:T(4,128)(2,1)} %param.7, pred[4,4]{1,0:T(4,128)(4,1)S(1)} %iota_compare_fusion), kind=kOutput, calls=%fused_computation.54 | convolution fusion | flops 16785152 | bytes 4195344 | tf_op jit(solution)/shard_map/tic,tjc->tij/dot_general | solution.py:81
  10.1 0.0 copy-done.7
  10.1 0.1 fusion.80
  10.2 0.1 add.132
  10.2 0.1 fusion.79
  10.3 0.1 add.164
  10.4 0.0 copy-done.8
  10.4 0.6 fusion.78
  11.0 0.0 copy-done.6
  11.1 33.9 %all_gather.21 = f32[24,4,2048]{2,0,1:T(8,128)S(1)} all-gather(f32[24,4,256]{2,0,1:T(8,128)S(1)} %copy.16), channel_id=1, replica_groups=mesh['dp'=8,'mp'=4] {'dp'}, dimensions={2}, use_global_device_ids=true | all-gather | bytes 884736 | tf_op jit(solution)/shard_map/all_gather | solution.py:75
  45.0 32.1 %all_gather.18 = f32[20,4,2048]{2,0,1:T(8,128)S(1)} all-gather(f32[20,4,256]{2,0,1:T(8,128)S(1)} %copy.10), channel_id=1, replica_groups=mesh['dp'=8,'mp'=4] {'dp'}, dimensions={2}, use_global_device_ids=true | all-gather | bytes 737280 | tf_op jit(solution)/shard_map/all_gather | solution.py:74
  77.1 9.2 %convolution_bitcast_fusion = f32[256,20]{0,1:T(8,128)S(1)} fusion(f32[20,4,2048]{2,0,1:T(8,128)S(1)} %all_gather.18, bf16[256,4,2048]{2,1,0:T(4,128)(2,1)} %param.7), kind=kOutput, calls=%fused_computation.56 | convolution fusion | flops 503316480 | bytes 4870144 | tf_op jit(solution)/shard_map/tic,kic->tk/dot_general | solution.py:78
  86.3 5.5 %all-gather = f32[1024,21]{0,1:T(8,128)S(1)} all-gather(f32[256,21]{0,1:T(8,128)S(1)} %pad_maximum_fusion.5), channel_id=2, replica_groups=mesh['dp'=8,'mp'=4] {'mp'}, dimensions={0}, use_global_device_ids=true | all-gather | bytes 107520 | tf_op jit(solution)/shard_map/all_gather | solution.py:20
  91.8 0.1 reduce_sum.263
  91.9 0.8 fusion.56
  92.7 0.7 slice_multiply_fusion.1
  93.4 0.1 fusion.74
  93.8 0.0 copy-start.4
  93.8 4.6 %copy.11 = bf16[256,4,2048]{2,0,1:T(8,128)(2,1)S(1)} copy(bf16[256,4,2048]{2,1,0:T(4,128)(2,1)} %param.7) | data formatting | bytes 8388608 | tf_op args[0]
  98.4 2.3 %fusion.13 = (f32[256,2048]{1,0:T(8,128)S(1)}, f32[256,2048]{1,0:T(8,128)S(1)}) fusion(bf16[256,2048]{1,0:T(8,128)(2,1)S(1)} %copy-done.4, f32[256]{0:T(256)S(1)} %bitcast.139, f32[256]{0:T(256)S(1)} %bitcast.140, f32[256]{0:T(256)S(1)} %bitcast.141, f32[256]{0:T(256)S(1)} %bitcast.134, f32[256]{0:T(256)S(1)} %bitcast.144, ...), kind=kLoop, calls=%fused_computation.35 | loop fusion | flops 12058624 | bytes 9447424 | tf_op jit(solution)/shard_map/add | solution.py:58
  100.6 2.3 %fusion.21 = (f32[256,2048]{1,0:T(8,128)S(1)}, f32[256,2048]{1,0:T(8,128)S(1)}) fusion(bf16[256,2048]{1,0:T(8,128)(2,1)S(1)} %copy-done.4, f32[256]{0:T(256)S(1)} %bitcast.130, f32[256]{0:T(256)S(1)} %bitcast.131, f32[256]{0:T(256)S(1)} %bitcast.132, f32[256]{0:T(256)S(1)} %bitcast.133, f32[256]{0:T(256)S(1)} %bitcast.143, ...), kind=kLoop, calls=%fused_computation.43 | loop fusion | flops 12058624 | bytes 9447424 | tf_op jit(solution)/shard_map/add | solution.py:58
  102.9 0.0 copy-start.3
  103.0 6.6 %fusion.29 = f32[256,24]{0,1:T(8,128)S(1)} fusion(f32[24,4,2048]{2,0,1:T(8,128)S(1)} %all_gather.21, f32[256,1,2048]{2,0,1:T(8,128)S(1)} %bitcast.115, f32[256,1,2048]{2,0,1:T(8,128)S(1)} %bitcast.112, f32[256,1,2048]{2,0,1:T(8,128)S(1)} %bitcast.109, f32[256,1,2048]{2,0,1:T(8,128)S(1)} %bitcast.106), kind=kOutput, calls=%fused_computation.55 | convolution fusion | flops 610271232 | bytes 9199616 | tf_op jit(solution)/shard_map/tic,kic->tk/dot_general | solution.py:95
  109.6 0.9 multiply_reduce_fusion
  110.5 5.6 %all-gather.1 = f32[1024,25]{0,1:T(8,128)S(1)} all-gather(f32[256,25]{0,1:T(8,128)S(1)} %pad_maximum_fusion.4), channel_id=3, replica_groups=mesh['dp'=8,'mp'=4] {'mp'}, dimensions={0}, use_global_device_ids=true | all-gather | bytes 128000 | tf_op jit(solution)/shard_map/all_gather | solution.py:20
  116.1 0.1 reshape.110
  116.2 0.1 reduce_sum.277
  116.3 1.4 fusion.45
  117.7 0.6 slice_multiply_fusion
  118.3 0.1 fusion.72
  118.4 0.1 divide_reduce_fusion
  118.5 0.1 divide_reduce_fusion.6
  118.6 0.1 divide_reduce_fusion.5
  118.7 0.1 divide_reduce_fusion.4
  118.8 0.1 divide_reduce_fusion.3
  118.9 0.1 divide_reduce_fusion.2
  119.1 0.7 exponential_divide_fusion
  119.8 0.6 pad_maximum_fusion.6
  120.4 4.9 %multiply_reduce_fusion.1 = (f32[256]{0:T(256)S(1)}, f32[256,2048]{1,0:T(8,128)}) fusion(f32[256,2048]{1,0:T(8,128)} %copy-done.3, f32[256]{0:T(256)S(1)} %bitcast.147, f32[256,2048]{1,0:T(8,128)} %copy-done.2, f32[256]{0:T(256)S(1)} %bitcast.148, f32[256,2048]{1,0:T(8,128)} %copy-done, f32[256]{0:T(256)S(1)} %bitcast.149, ...), kind=kLoop, calls=%fused_computation.49 | loop fusion | flops 4718336 | bytes 10490880 | tf_op jit(solution)/shard_map/reduce_sum | solution.py:111
  125.3 7.1 %psum.7 = f32[256]{0:T(256)S(1)} all-reduce(f32[256]{0:T(256)S(1)} %get-tuple-element.6), channel_id=1, replica_groups=mesh['dp'=8,'mp'=4] {'mp'}, use_global_device_ids=true, to_apply=%region_17.18 | all-reduce | flops 256 | bytes 2048 | tf_op jit(solution)/shard_map/psum | solution.py:111
  132.4 0.0 copy-done.9
  132.4 3.0 %multiply_convert_fusion = bf16[256,2048]{1,0:T(8,128)(2,1)} fusion(f32[256,2048]{1,0:T(8,128)} %get-tuple-element.7, f32[2048]{0:T(1024)S(1)} %copy-done.9, f32[256]{0:T(256)S(1)} %add_sqrt_fusion), kind=kLoop, calls=%fused_computation.48 | loop fusion | flops 1572864 | bytes 3154944 | tf_op jit(solution)/shard_map/convert_element_type | solution.py:112
  135.4 2.6 %fusion.27 = bf16[256,4,2048]{2,0,1:T(8,128)(2,1)S(1)} fusion(f32[256,1,2048]{2,0,1:T(8,128)} %bitcast.117, f32[256,1,2048]{2,0,1:T(8,128)} %bitcast.114, f32[256,1,2048]{2,0,1:T(8,128)S(1)} %bitcast.111, f32[256,1,2048]{2,0,1:T(8,128)S(1)} %bitcast.108), kind=kLoop, calls=%fused_computation.52 | loop fusion | flops 6291456 | bytes 12582912 | tf_op jit(solution)/shard_map/convert_element_type | solution.py:94
  138.0 5.3 %copy.17 = bf16[256,4,2048]{2,1,0:T(4,128)(2,1)} copy(bf16[256,4,2048]{2,0,1:T(8,128)(2,1)S(1)} %fusion.27) | data formatting | bytes 8388608
  (37 shorter events, 0.5 us)
Async XLA Ops:
  0.6 9.4 %copy-start.7 = (f32[44]{0:T(128)S(1)}, f32[44]{0:T(128)}, u32[]{:S(2)}) copy-start(f32[44]{0:T(128)} %param.11) | copy-start | bytes 532
  0.7 9.8 %copy-start.8 = (f32[5]{0:T(128)S(1)}, f32[5]{0:T(128)}, u32[]{:S(2)}) copy-start(f32[5]{0:T(128)} %param.12) | copy-start | bytes 64
  0.7 10.4 %copy-start.6 = (f32[20,4,256]{2,1,0:T(4,128)S(1)}, f32[20,4,256]{2,1,0:T(4,128)}, u32[]{:S(2)}) copy-start(f32[20,4,256]{2,1,0:T(4,128)} %param.9) | copy-start | bytes 245764
  0.7 10.4 %copy-start.5 = (f32[24,4,256]{2,1,0:T(4,128)S(1)}, f32[24,4,256]{2,1,0:T(4,128)}, u32[]{:S(2)}) copy-start(f32[24,4,256]{2,1,0:T(4,128)} %param.10) | copy-start | bytes 294916
  93.8 4.6 %copy-start.4 = (bf16[256,2048]{1,0:T(8,128)(2,1)S(1)}, bf16[256,2048]{1,0:T(8,128)(2,1)}, u32[]{:S(2)}) copy-start(bf16[256,2048]{1,0:T(8,128)(2,1)} %param.8) | copy-start | bytes 3145732
  100.6 8.9 %copy-start = (f32[256,2048]{1,0:T(8,128)}, f32[256,2048]{1,0:T(8,128)S(1)}, u32[]{:S(2)}) copy-start(f32[256,2048]{1,0:T(8,128)S(1)} %get-tuple-element.11) | copy-start | bytes 6291460
  102.9 6.6 %copy-start.2 = (f32[256,2048]{1,0:T(8,128)}, f32[256,2048]{1,0:T(8,128)S(1)}, u32[]{:S(2)}) copy-start(f32[256,2048]{1,0:T(8,128)S(1)} %get-tuple-element.12) | copy-start | bytes 6291460
  102.9 6.6 %copy-start.3 = (f32[256,2048]{1,0:T(8,128)}, f32[256,2048]{1,0:T(8,128)S(1)}, u32[]{:S(2)}) copy-start(f32[256,2048]{1,0:T(8,128)S(1)} %get-tuple-element.13) | copy-start | bytes 6291460
  120.4 12.0 %copy-start.9 = (f32[2048]{0:T(1024)S(1)}, f32[2048]{0:T(1024)}, u32[]{:S(2)}) copy-start(f32[2048]{0:T(1024)} %param.13) | copy-start | bytes 24580
  132.3 3.1 %copy-start.1 = (f32[256,2048]{1,0:T(8,128)S(1)}, f32[256,2048]{1,0:T(8,128)}, u32[]{:S(2)}) copy-start(f32[256,2048]{1,0:T(8,128)} %copy-done) | copy-start | bytes 6291460
